TPU v7x, 32 devices: a whole 2x2x4 slice. The times are simulated.
32 devices in a mesh: row: 4 (over z), col: 8 (over y, x, core).
Axes of the slice: x: 2, y: 2, z: 4, core: 2. Of those that a mesh axis runs over, the one named last changes fastest.
Arguments:
- matrix: float32 [8192, 8192], P('row', 'col'), may hold values from -2.5 to 2.5
Outputs:
- squared: float32 [8192, 8192], P('row', 'col')
- frob: float32 [], replicated
All inputs are finite; a program needn't handle non-finite values.
Results may differ from a plain program's by a relative error of at most 0.0001.
Values sent between devices are 32-bit elements; how exact they have to be, the bound alone decides.
A program may use at most 64 MiB of HBM per device.

v0:
```python
import jax
import jax.numpy as jnp
from jax import lax
from jax.sharding import PartitionSpec as P

KP = 256


def broadcast(value, axis, source):
    kept = jnp.where(lax.axis_index(axis) == source, value, 0).astype(value.dtype)
    return lax.psum(kept, axis)


def offsets(matrix, step):
    row_block = matrix.shape[0]
    col_block = matrix.shape[1]
    total = row_block * lax.axis_size("row")
    start = step * (total // 4)
    return (start // col_block, start % col_block, start // row_block, start % row_block)


def fetch_rows(matrix, step):
    col_owner, local_col, row_owner, local_row = offsets(matrix, step)
    return broadcast(matrix[local_row : local_row + KP, :], "row", row_owner)


def product(left, right):
    return jnp.dot(left, right, preferred_element_type=jnp.float32, precision=lax.Precision.HIGHEST)


def body(matrix):
    column_index = lax.axis_index("col")
    slots = []
    for step in range(4):
        col_owner, local_col, row_owner, local_row = offsets(matrix, step)
        panel = matrix[:, local_col : local_col + KP]
        slots.append(jnp.where(column_index == col_owner, panel, jnp.zeros_like(panel)))
    stacked = lax.psum(jnp.concatenate(slots, axis=1), "col")
    rights = jnp.concatenate([fetch_rows(matrix, step) for step in range(4)], axis=0)
    squared = product(stacked, rights)
    total = lax.psum(jnp.sum(squared * squared), ("row", "col"))
    order_size = matrix.shape[0] * lax.axis_size("row")
    frob = jnp.sqrt(total) / order_size
    return (squared, frob)


def solution(mesh):
    placed = (P("row", "col"),)
    return jax.shard_map(
        body, mesh=mesh, in_specs=placed, out_specs=(P("row", "col"), P()), check_vma=False
    )
```

profile of v0, /device:TPU:0, one launch (start us, length us, event | category | flops | bytes accessed | tf_op | source)
XLA Modules:
  0.0 378.5 jit_solution(3300064162137872236)
XLA Ops:
  7.2 0.0 all-reduce.6.cloned.1.call-start
  7.2 3.4 slice_select_fusion.7
  10.7 0.0 all-reduce.6.cloned.1.call-update
  10.7 0.0 all-reduce.4.cloned.1.call-start
  10.7 2.2 slice_select_fusion.3
  13.0 4.1 %pad_maximum_fusion = f32[2048,1024]{1,0:T(8,128)} fusion(f32[2048,256]{1,0:T(8,128)S(1)} %get-tuple-element.13, f32[2048,256]{1,0:T(8,128)S(1)} %get-tuple-element.12, f32[2048,256]{1,0:T(8,128)S(1)} %get-tuple-element.11, f32[2048,256]{1,0:T(8,128)S(1)} %get-tuple-element.10), kind=kLoop, calls=%fused_computation | loop fusion | flops 6291456 | bytes 16777216 | tf_op jit(solution)/shard_map/concatenate | solution.py:38
  17.0 0.0 all-reduce.4.cloned.1.call-update
  17.1 151.5 %all-reduce.6.cloned.1.call-done = (f32[256,1024]{1,0:T(8,128)}, f32[256,1024]{1,0:T(8,128)}, f32[256,1024]{1,0:T(8,128)}, f32[256,1024]{1,0:T(8,128)}) async-done(((f32[256,1024]{1,0:T(8,128)}, f32[256,1024]{1,0:T(8,128)}, f32[256,1024]{1,0:T(8,128)}, f32[256,1024]{1,0:T(8,128)}), (f32[256,1024]{1,0:T(8,128)}, f32[256,1024]{1,0:T(8,128)}, f32[256,1024]{1,0:T(8,128)}, ...) | async-done | bytes 4194320 | tf_op jit(solution)/shard_map/psum | solution.py:11
  168.6 129.3 %all-reduce.4.cloned.1.call-done = f32[2048,1024]{1,0:T(8,128)} async-done(((f32[2048,1024]{1,0:T(8,128)}), f32[2048,1024]{1,0:T(8,128)}) %all-reduce.4.cloned.1.call-update) | async-done | bytes 8388624 | tf_op jit(solution)/shard_map/psum | solution.py:38
  297.8 32.3 %multiply_reduce_fusion = (f32[]{:T(128)}, f32[2048,1024]{1,0:T(8,128)}) fusion(f32[2048,1024]{1,0:T(8,128)} %all-reduce.4.cloned.1.call-done, f32[256,1024]{1,0:T(8,128)} %get-tuple-element.2, f32[256,1024]{1,0:T(8,128)} %get-tuple-element.3, f32[256,1024]{1,0:T(8,128)} %get-tuple-element.4, f32[256,1024]{1,0:T(8,128)} %get-tuple-element.5), kind=kOutput, calls=%fused_computation.1 | convolution fusion | flops 25777143808 | bytes 20971524 | tf_op jit(solution)/shard_map/dot_general | solution.py:28
  330.2 39.6 %psum.47 = f32[]{:T(128)} all-reduce(f32[]{:T(128)} %get-tuple-element.14), channel_id=1, replica_groups=mesh['row'=4,'col'=8] {'row','col'}, use_global_device_ids=true, to_apply=%region_6.7 | all-reduce | flops 1 | bytes 8 | tf_op jit(solution)/shard_map/psum | solution.py:41
Async XLA Ops:
  7.2 161.4 %all-reduce.6.cloned.1.call-start = ((), (), s32[]{:S(2)}) async-start(), calls=%async_computation.1 | async-start | bytes 8388608 | tf_op jit(solution)/shard_map/psum | solution.py:11
  10.7 287.2 %all-reduce.4.cloned.1.call-start = ((), (), s32[]{:S(2)}) async-start(), calls=%async_computation | async-start | bytes 16777216 | tf_op jit(solution)/shard_map/psum | solution.py:38
Sparse Core Ops, SparseCore 0:
  10.8 157.7 all-reduce.5
  172.6 125.1 all-reduce.3
where the time goes:
time: 379 us; the launch traced here: 378 us
  waiting for transfers between devices  281 us (74%)
  blocking collectives  39.6 us (10%)
  matrix products  32.3 us (9%)
  between operations  15.9 us (4%)
  other arithmetic  9.73 us (3%)
    psum x1, waiting for transfers between devices, broadcast(): return lax.psum(kept, axis)  152 us
    psum x1, waiting for transfers between devices, body(): stacked = lax.psum(jnp.concatenate(slots, axis=1), 'col')  129 us
    psum x1, blocking collectives, body(): total = lax.psum(jnp.sum(squared * squared), ('row', 'col'))  39.6 us
    dot_general x1, matrix products, product(): jnp.dot(left, right, preferred_element_type=jnp.float32, precision=lax.Pr...  32.3 us
  transfers between devices with their start and end apart: 2, of which 2 were waited for; matrix products, arithmetic and copies ran while one was open for 2% of the time, Pallas kernels for 0%

commit v1 on v0

v1 whole, which is shorter than its diff:
```python
import functools

import jax
import jax.numpy as jnp
from jax import lax
from jax.experimental import pallas as pl
from jax.experimental.pallas import tpu as pltpu
from jax.sharding import PartitionSpec as P

KP = 256
PANELS = 4
MESH = pl.DeviceIdType.MESH


def kernel(
    rows_n, cols_n, order, pieces, x_ref, out_ref, frob_ref, right, left, high, low, part_col, part_row,
    local_sem, z_recv, z_up, z_down, pair_send, pair_recv, hop_send, hop_recv, relay_send, relay_recv,
    col_send, col_recv, row_send, row_recv,
):
    row = lax.axis_index("row")
    col = lax.axis_index("col")
    chip = col // 2
    core = col % 2
    partner = chip * 2 + 1 - core
    row_block, col_block = out_ref.shape
    half = row_block // 2
    width = col_block // pieces

    barrier = pltpu.get_barrier_semaphore()
    for d in range(1, cols_n):
        pl.semaphore_signal(barrier, inc=1, device_id=(row, lax.rem(col + d, cols_n)), device_id_type=MESH)
    for d in range(1, rows_n):
        pl.semaphore_signal(barrier, inc=1, device_id=(lax.rem(row + d, rows_n), col), device_id_type=MESH)
    pl.semaphore_wait(barrier, rows_n + cols_n - 2)

    def columns(j):
        return pl.ds(pl.multiple_of(j * width, width), width)

    def z_copy(s, j, sems, target, own):
        view = right.at[s, :, columns(j)]
        source = x_ref.at[pl.ds(0, KP), columns(j)] if own else view
        return pltpu.make_async_remote_copy(
            src_ref=source, dst_ref=view, send_sem=sems.at[s, j], recv_sem=z_recv.at[s, j],
            device_id=(target, col), device_id_type=MESH,
        )

    above = lax.min(row + 1, rows_n - 1)
    below = lax.max(row - 1, 0)
    has_above = row < rows_n - 1
    has_below = row > 0

    def start_own(j, carry):
        @pl.when(has_above)
        def _():
            z_copy(row, j, z_up, above, True).start()

        @pl.when(has_below)
        def _():
            z_copy(row, j, z_down, below, True).start()

        return carry

    lax.fori_loop(0, pieces, start_own, 0)

    def pair_copy():
        return pltpu.make_async_remote_copy(
            src_ref=x_ref.at[:, pl.ds(0, KP)], dst_ref=left.at[chip], send_sem=pair_send, recv_sem=pair_recv,
            device_id=(row, partner), device_id_type=MESH,
        )

    def flip(q, d):
        hi, lo = q // 2, q % 2
        hi = hi if d < 2 else 1 - hi
        lo = lo if d % 2 == 0 else 1 - lo
        return hi * 2 + lo

    def hop_copy(d, h):
        rows = pl.ds(h * half, half)
        return pltpu.make_async_remote_copy(
            src_ref=x_ref.at[rows, pl.ds(0, KP)], dst_ref=left.at[chip, rows, :],
            send_sem=hop_send.at[d, h], recv_sem=hop_recv.at[chip],
            device_id=(row, flip(chip, d) * 2 + h), device_id_type=MESH,
        )

    @pl.when(core == 0)
    def _():
        for d in (1, 2, 3):
            for h in (0, 1):
                hop_copy(d, h).start()
        pair_copy().start()

    own_right = pltpu.make_async_copy(x_ref.at[pl.ds(0, KP), :], right.at[row], local_sem.at[0])
    own_left = pltpu.make_async_copy(x_ref.at[:, pl.ds(0, KP)], left.at[chip], local_sem.at[1])
    own_right.start()

    @pl.when(core == 0)
    def _():
        own_left.start()

    tile = 256
    tiles = row_block // tile

    def clear(i, carry):
        out_ref[pl.ds(pl.multiple_of(i * tile, tile), tile), :] = jnp.zeros((tile, col_block), jnp.float32)
        return carry

    lax.fori_loop(0, tiles, clear, 0)

    def split(s):
        def one(i, carry):
            rows = pl.ds(pl.multiple_of(i * tile, tile), tile)
            value = left[s, rows, :]
            head = value.astype(jnp.bfloat16)
            high[s, rows, :] = head
            low[s, rows, :] = (value - head.astype(jnp.float32)).astype(jnp.bfloat16)
            return carry

        lax.fori_loop(0, tiles, one, 0)

    def multiply(s, j):
        cols = columns(j)
        value = right[s, :, cols]
        head = value.astype(jnp.bfloat16)
        tail = (value - head.astype(jnp.float32)).astype(jnp.bfloat16)

        def one(i, carry):
            rows = pl.ds(pl.multiple_of(i * tile, tile), tile)
            a, b = high[s, rows, :], low[s, rows, :]
            dot = functools.partial(jnp.dot, preferred_element_type=jnp.float32)
            out_ref[rows, cols] += dot(a, head) + (dot(a, tail) + dot(b, head))
            return carry

        lax.fori_loop(0, tiles, one, 0)

    def receive(k, j):
        @pl.when(row >= k)
        def _():
            s = lax.max(row - k, 0)
            z_copy(s, j, z_up, above, False).wait_recv()

            @pl.when(has_above)
            def _():
                z_copy(s, j, z_up, above, False).start()

        @pl.when(row + k < rows_n)
        def _():
            s = lax.min(row + k, rows_n - 1)
            z_copy(s, j, z_down, below, False).wait_recv()

            @pl.when(has_below)
            def _():
                z_copy(s, j, z_down, below, False).start()

    def compute(k, j):
        @pl.when(row >= k)
        def _():
            multiply(lax.max(row - k, 0), j)

        @pl.when(row + k < rows_n)
        def _():
            multiply(lax.min(row + k, rows_n - 1), j)

    mine = pl.ds(pl.multiple_of(core * half, half), half)
    other = pl.ds(pl.multiple_of((1 - core) * half, half), half)

    def relay_copy(s, rows):
        return pltpu.make_async_remote_copy(
            src_ref=left.at[s, rows, :], dst_ref=left.at[s, rows, :], send_sem=relay_send.at[s],
            recv_sem=relay_recv.at[s], device_id=(row, partner), device_id_type=MESH,
        )

    def hop_arrival(s):
        view = left.at[s, mine, :]
        return pltpu.make_async_remote_copy(
            src_ref=view, dst_ref=view, send_sem=hop_send.at[0, 0], recv_sem=hop_recv.at[s],
            device_id=(row, partner), device_id_type=MESH,
        )

    def relay(distances):
        for d in distances:
            s = flip(chip, d)
            hop_arrival(s).wait_recv()
            relay_copy(s, mine).start()
        for d in distances:
            s = flip(chip, d)
            relay_copy(s, other).wait_recv()
            relay_copy(s, mine).wait_send()
            split(s)

    own_right.wait()

    @pl.when(core == 0)
    def _():
        own_left.wait()

    @pl.when(core == 1)
    def _():
        pair_copy().wait_recv()

    split(chip)

    def step(k, work):
        def one(j, carry):
            receive(k, j)
            if work:
                compute(k, j)
            return carry

        lax.fori_loop(0, pieces, one, 0)

    step(1, False)
    relay((1, 2))
    step(2, False)
    relay((3,))

    def early(j, carry):
        multiply(row, j)
        compute(1, j)
        compute(2, j)
        return carry

    lax.fori_loop(0, pieces, early, 0)

    def last(j, total):
        for k in range(3, rows_n):
            receive(k, j)
            compute(k, j)
        cols = columns(j)

        def one(i, acc):
            value = out_ref[pl.ds(pl.multiple_of(i * tile, tile), tile), cols]
            value = value * value
            return acc + jnp.sum(value.reshape(tile // 8, 8, width), axis=0)

        return lax.fori_loop(0, tiles, one, total)

    total = lax.fori_loop(0, pieces, last, jnp.zeros((8, width), jnp.float32))
    part_col[col] = sum(total[:, i * 128 : (i + 1) * 128] for i in range(width // 128))

    def drain(j, carry):
        @pl.when(has_above)
        def _():
            z_copy(row, j, z_up, above, True).wait_send()

        @pl.when(has_below)
        def _():
            z_copy(row, j, z_down, below, True).wait_send()

        for k in range(1, rows_n):
            @pl.when(jnp.logical_and(row >= k, has_above))
            def _():
                z_copy(lax.max(row - k, 0), j, z_up, above, False).wait_send()

            @pl.when(jnp.logical_and(row + k < rows_n, has_below))
            def _():
                z_copy(lax.min(row + k, rows_n - 1), j, z_down, below, False).wait_send()

        return carry

    lax.fori_loop(0, pieces, drain, 0)

    @pl.when(core == 0)
    def _():
        for d in (1, 2, 3):
            for h in (0, 1):
                hop_copy(d, h).wait_send()
        pair_copy().wait_send()

    def spread(part, place, count, send, recv, device):
        def copy(d, slot):
            return pltpu.make_async_remote_copy(
                src_ref=part.at[slot], dst_ref=part.at[slot], send_sem=send.at[d], recv_sem=recv.at[slot],
                device_id=device(lax.rem(place + d, count)), device_id_type=MESH,
            )

        for d in range(1, count):
            copy(d, place).start()
        for d in range(1, count):
            copy(d, lax.rem(place + d, count)).wait_recv()
        for d in range(1, count):
            copy(d, place).wait_send()

    spread(part_col, col, cols_n, col_send, col_recv, lambda c: (row, c))
    part_row[row] = jnp.sum(part_col[...], axis=0)
    spread(part_row, row, rows_n, row_send, row_recv, lambda r: (r, col))
    full = jnp.sum(jnp.sum(part_row[...], axis=0), keepdims=True)
    frob_ref[...] = jnp.sqrt(full) / order


def fused(rows_n, cols_n, matrix):
    row_block, col_block = matrix.shape
    order = row_block * rows_n
    pieces = max(1, col_block // 256)
    dma = pltpu.SemaphoreType.DMA
    vmem = pl.BlockSpec(memory_space=pltpu.VMEM)
    squared, frob = pl.pallas_call(
        functools.partial(kernel, rows_n, cols_n, order, pieces),
        out_shape=(
            jax.ShapeDtypeStruct((row_block, col_block), jnp.float32),
            jax.ShapeDtypeStruct((1, 1), jnp.float32),
        ),
        in_specs=[pl.BlockSpec(memory_space=pltpu.HBM)],
        out_specs=(vmem, vmem),
        scratch_shapes=[
            pltpu.VMEM((PANELS, KP, col_block), jnp.float32),
            pltpu.VMEM((PANELS, row_block, KP), jnp.float32),
            pltpu.VMEM((PANELS, row_block, KP), jnp.bfloat16),
            pltpu.VMEM((PANELS, row_block, KP), jnp.bfloat16),
            pltpu.VMEM((cols_n, 8, 128), jnp.float32),
            pltpu.VMEM((rows_n, 8, 128), jnp.float32),
            dma((2,)), dma((PANELS, pieces)), dma((PANELS, pieces)), dma((PANELS, pieces)),
            dma(()), dma(()), dma((PANELS, 2)), dma((PANELS,)), dma((PANELS,)), dma((PANELS,)),
            dma((cols_n,)), dma((cols_n,)), dma((rows_n,)), dma((rows_n,)),
        ],
        compiler_params=pltpu.CompilerParams(
            collective_id=0, has_side_effects=True, vmem_limit_bytes=60 * 1024 * 1024
        ),
    )(matrix)
    return squared, frob.reshape(())


def broadcast(value, axis, source):
    kept = jnp.where(lax.axis_index(axis) == source, value, 0).astype(value.dtype)
    return lax.psum(kept, axis)


def offsets(matrix, step):
    row_block = matrix.shape[0]
    col_block = matrix.shape[1]
    total = row_block * lax.axis_size("row")
    start = step * (total // PANELS)
    return (start // col_block, start % col_block, start // row_block, start % row_block)


def fetch_rows(matrix, step):
    col_owner, local_col, row_owner, local_row = offsets(matrix, step)
    return broadcast(matrix[local_row : local_row + KP, :], "row", row_owner)


def product(left, right):
    return jnp.dot(left, right, preferred_element_type=jnp.float32, precision=lax.Precision.HIGHEST)


def general(matrix):
    column_index = lax.axis_index("col")
    slots = []
    for step in range(PANELS):
        col_owner, local_col, row_owner, local_row = offsets(matrix, step)
        panel = matrix[:, local_col : local_col + KP]
        slots.append(jnp.where(column_index == col_owner, panel, jnp.zeros_like(panel)))
    stacked = lax.psum(jnp.concatenate(slots, axis=1), "col")
    rights = jnp.concatenate([fetch_rows(matrix, step) for step in range(PANELS)], axis=0)
    squared = product(stacked, rights)
    total = lax.psum(jnp.sum(squared * squared), ("row", "col"))
    order_size = matrix.shape[0] * lax.axis_size("row")
    frob = jnp.sqrt(total) / order_size
    return (squared, frob)


def solution(mesh):
    rows_n, cols_n = mesh.shape["row"], mesh.shape["col"]
    if rows_n == PANELS and cols_n == 2 * PANELS:
        body = functools.partial(fused, rows_n, cols_n)
    else:
        body = general
    return jax.shard_map(
        body, mesh=mesh, in_specs=(P("row", "col"),), out_specs=(P("row", "col"), P()), check_vma=False
    )
```

time: 379 us -> 115 us (0.30)
  waiting for transfers between devices: 281 us -> 0 us
  Pallas kernels: 0 us -> 104 us
  blocking collectives: 39.6 us -> 0 us
  matrix products: 32.3 us -> 0 us
  between operations: 15.9 us -> 2.39 us
  other arithmetic: 9.73 us -> 0 us
  local copies, waits for them, and re-layouts: 0 us -> 8.44 us
    psum x2 -> x0, waiting for transfers between devices: 281 us -> none  [the longest x1 152 us: broadcast(): return lax.psum(kept, axis)]
    pallas_call x0 -> x1, Pallas kernels: none -> 104 us  [fused(): pl.pallas_call(functools.partial(kernel, rows_n, cols_n, order, pieces),...]
    psum x1 -> x0, blocking collectives: 39.6 us -> none  [body(): total = lax.psum(jnp.sum(squared * squared), ('row', 'col'))]
    dot_general x1 -> x0, matrix products: 32.3 us -> none  [product(): jnp.dot(left, right, preferred_element_type=jnp.float32, precision=lax.Pr...]
    unnamed x0 -> x1, local copies, waits for them, and re-layouts: none -> 8.44 us
    select_n x2 -> x0, other arithmetic: 5.67 us -> none  [the longest x1 3.43 us: broadcast(): jnp.where(lax.axis_index(axis) == source, value, 0).astype(value.dtype)]
    concatenate x1 -> x0, other arithmetic: 4.06 us -> none  [body(): stacked = lax.psum(jnp.concatenate(slots, axis=1), 'col')]
  transfers between devices with their start and end apart: 2 -> 0, of which waited for: 2 -> 0; matrix products, arithmetic and copies ran while one was open for 2% -> 0% of each run, Pallas kernels for 0% -> 0%
where the time goes in v1:
time: 115 us
  Pallas kernels  104 us (90%)
  local copies, waits for them, and re-layouts  8.44 us (7%)
  between operations  2.39 us (2%)
    pallas_call x1, Pallas kernels, fused(): pl.pallas_call(functools.partial(kernel, rows_n, cols_n, order, pieces),...  104 us
    unnamed x1, local copies, waits for them, and re-layouts  8.44 us

profile of v1, /device:TPU:0, one launch (start us, length us, event | category | flops | bytes accessed | tf_op | source)
XLA Modules:
  0.0 114.7 jit_solution(5505366946623183800)
XLA Ops:
  0.6 103.9 %shard_map.30 = (f32[2048,1024]{1,0:T(8,128)}, f32[1,1]{1,0:T(1,128)}) custom-call(f32[2048,1024]{1,0:T(8,128)} %x_ref.1), custom_call_target="tpu_custom_call" | custom-call | tf_op jit(solution)/shard_map/pallas_call | solution.py:296
  104.5 8.4 %copy.5 = f32[2048,1024]{1,0:T(8,128)} copy(f32[2048,1024]{1,0:T(8,128)} %get-tuple-element.8) | data formatting | bytes 16777216

commit v2 on v1

--- a/solution.py
+++ b/solution.py
@@ -9,11 +9,12 @@
 
 KP = 256
 PANELS = 4
+DOT = 1024
 MESH = pl.DeviceIdType.MESH
 
 
 def kernel(
-    rows_n, cols_n, order, pieces, x_ref, out_ref, frob_ref, right, left, high, low, part_col, part_row,
+    rows_n, cols_n, order, pieces, x_ref, out_ref, frob_ref, right, left, halves, weights, part_col, part_row,
     local_sem, z_recv, z_up, z_down, pair_send, pair_recv, hop_send, hop_recv, relay_send, relay_recv,
     col_send, col_recv, row_send, row_recv,
 ):
@@ -100,37 +101,39 @@
     tile = 256
     tiles = row_block // tile
 
-    def clear(i, carry):
-        out_ref[pl.ds(pl.multiple_of(i * tile, tile), tile), :] = jnp.zeros((tile, col_block), jnp.float32)
-        return carry
-
-    lax.fori_loop(0, tiles, clear, 0)
-
     def split(s):
         def one(i, carry):
             rows = pl.ds(pl.multiple_of(i * tile, tile), tile)
             value = left[s, rows, :]
             head = value.astype(jnp.bfloat16)
-            high[s, rows, :] = head
-            low[s, rows, :] = (value - head.astype(jnp.float32)).astype(jnp.bfloat16)
+            halves[s, rows, pl.ds(0, KP)] = head
+            halves[s, rows, pl.ds(KP, KP)] = (value - head.astype(jnp.float32)).astype(jnp.bfloat16)
             return carry
 
         lax.fori_loop(0, tiles, one, 0)
 
-    def multiply(s, j):
+    def multiply(first, count, j, add):
         cols = columns(j)
-        value = right[s, :, cols]
-        head = value.astype(jnp.bfloat16)
-        tail = (value - head.astype(jnp.float32)).astype(jnp.bfloat16)
+        for i in range(count):
+            value = right[first + i, :, cols]
+            head = value.astype(jnp.bfloat16)
+            weights[pl.ds(3 * KP * i, KP), :] = head
+            weights[pl.ds(3 * KP * i + KP, KP), :] = head
+            weights[pl.ds(3 * KP * i + 2 * KP, KP), :] = (value - head.astype(jnp.float32)).astype(jnp.bfloat16)
 
         def one(i, carry):
-            rows = pl.ds(pl.multiple_of(i * tile, tile), tile)
-            a, b = high[s, rows, :], low[s, rows, :]
-            dot = functools.partial(jnp.dot, preferred_element_type=jnp.float32)
-            out_ref[rows, cols] += dot(a, head) + (dot(a, tail) + dot(b, head))
+            rows = pl.ds(pl.multiple_of(i * DOT, DOT), DOT)
+            pieces_of = []
+            for p in range(count):
+                pieces_of += [halves[first + p, rows, :], halves[first + p, rows, pl.ds(0, KP)]]
+            value = jnp.dot(
+                jnp.concatenate(pieces_of, axis=1), weights[pl.ds(0, 3 * KP * count), :],
+                preferred_element_type=jnp.float32,
+            )
+            out_ref[rows, cols] = value + out_ref[rows, cols] if add else value
             return carry
 
-        lax.fori_loop(0, tiles, one, 0)
+        lax.fori_loop(0, row_block // DOT, one, 0)
 
     def receive(k, j):
         @pl.when(row >= k)
@@ -150,15 +153,6 @@
             @pl.when(has_below)
             def _():
                 z_copy(s, j, z_down, below, False).start()
-
-    def compute(k, j):
-        @pl.when(row >= k)
-        def _():
-            multiply(lax.max(row - k, 0), j)
-
-        @pl.when(row + k < rows_n)
-        def _():
-            multiply(lax.min(row + k, rows_n - 1), j)
 
     mine = pl.ds(pl.multiple_of(core * half, half), half)
     other = pl.ds(pl.multiple_of((1 - core) * half, half), half)
@@ -199,32 +193,31 @@
 
     split(chip)
 
-    def step(k, work):
+    def step(k):
         def one(j, carry):
             receive(k, j)
-            if work:
-                compute(k, j)
             return carry
 
         lax.fori_loop(0, pieces, one, 0)
 
-    step(1, False)
+    step(1)
     relay((1, 2))
-    step(2, False)
+    step(2)
     relay((3,))
 
+    low_end = row < rows_n // 2
+    first = jnp.where(low_end, 0, 1)
+    farthest = jnp.where(low_end, rows_n - 1, 0)
+
     def early(j, carry):
-        multiply(row, j)
-        compute(1, j)
-        compute(2, j)
+        multiply(first, PANELS - 1, j, False)
         return carry
 
     lax.fori_loop(0, pieces, early, 0)
 
     def last(j, total):
-        for k in range(3, rows_n):
-            receive(k, j)
-            compute(k, j)
+        receive(rows_n - 1, j)
+        multiply(farthest, 1, j, True)
         cols = columns(j)
 
         def one(i, acc):
@@ -296,7 +289,7 @@
     squared, frob = pl.pallas_call(
         functools.partial(kernel, rows_n, cols_n, order, pieces),
         out_shape=(
-            jax.ShapeDtypeStruct((row_block, col_block), jnp.float32),
+            pltpu.VMEM((row_block, col_block), jnp.float32),
             jax.ShapeDtypeStruct((1, 1), jnp.float32),
         ),
         in_specs=[pl.BlockSpec(memory_space=pltpu.HBM)],
@@ -304,8 +297,8 @@
         scratch_shapes=[
             pltpu.VMEM((PANELS, KP, col_block), jnp.float32),
             pltpu.VMEM((PANELS, row_block, KP), jnp.float32),
-            pltpu.VMEM((PANELS, row_block, KP), jnp.bfloat16),
-            pltpu.VMEM((PANELS, row_block, KP), jnp.bfloat16),
+            pltpu.VMEM((PANELS, row_block, 2 * KP), jnp.bfloat16),
+            pltpu.VMEM((3 * KP * (PANELS - 1), col_block // pieces), jnp.bfloat16),
             pltpu.VMEM((cols_n, 8, 128), jnp.float32),
             pltpu.VMEM((rows_n, 8, 128), jnp.float32),
             dma((2,)), dma((PANELS, pieces)), dma((PANELS, pieces)), dma((PANELS, pieces)),
@@ -313,7 +306,7 @@
             dma((cols_n,)), dma((cols_n,)), dma((rows_n,)), dma((rows_n,)),
         ],
         compiler_params=pltpu.CompilerParams(
-            collective_id=0, has_side_effects=True, vmem_limit_bytes=60 * 1024 * 1024
+            collective_id=0, has_side_effects=True, vmem_limit_bytes=52 * 1024 * 1024
         ),
     )(matrix)
     return squared, frob.reshape(())

time: 115 us -> 89.9 us (0.78)
  Pallas kernels: 104 us -> 84 us
  local copies, waits for them, and re-layouts: 8.44 us -> 3.4 us
    pallas_call x1, Pallas kernels: 104 us -> 84 us  [fused(): pl.pallas_call(functools.partial(kernel, rows_n, cols_n, order, pieces),...]
    unnamed x1, local copies, waits for them, and re-layouts: 8.44 us -> 3.4 us
where the time goes in v2:
time: 89.9 us; the launch traced here: 89.7 us
  Pallas kernels  84 us (93%)
  local copies, waits for them, and re-layouts  3.4 us (4%)
  between operations  2.33 us (3%)
    pallas_call x1, Pallas kernels, fused(): pl.pallas_call(functools.partial(kernel, rows_n, cols_n, order, pieces),...  84 us
    unnamed x1, local copies, waits for them, and re-layouts  3.4 us

profile of v2, /device:TPU:0, one launch (start us, length us, event | category | flops | bytes accessed | tf_op | source)
XLA Modules:
  0.0 89.7 jit_solution(8444405356182739294)
XLA Ops:
  0.6 84.0 %shard_map.30 = (f32[2048,1024]{1,0:T(8,128)S(1)}, f32[1,1]{1,0:T(1,128)}) custom-call(f32[2048,1024]{1,0:T(8,128)} %x_ref.1), custom_call_target="tpu_custom_call" | custom-call | tf_op jit(solution)/shard_map/pallas_call | solution.py:289
  84.6 3.4 %copy.5 = f32[2048,1024]{1,0:T(8,128)} copy(f32[2048,1024]{1,0:T(8,128)S(1)} %get-tuple-element.6) | data formatting | bytes 16777216

commit v3 on v2

--- a/solution.py
+++ b/solution.py
@@ -101,6 +101,12 @@
     tile = 256
     tiles = row_block // tile
 
+    def clear(i, carry):
+        out_ref[pl.ds(pl.multiple_of(i * tile, tile), tile), :] = jnp.zeros((tile, col_block), jnp.float32)
+        return carry
+
+    lax.fori_loop(0, tiles, clear, 0)
+
     def split(s):
         def one(i, carry):
             rows = pl.ds(pl.multiple_of(i * tile, tile), tile)
@@ -202,18 +208,31 @@
 
     step(1)
     relay((1, 2))
-    step(2)
-    relay((3,))
-
     low_end = row < rows_n // 2
     first = jnp.where(low_end, 0, 1)
     farthest = jnp.where(low_end, rows_n - 1, 0)
-
-    def early(j, carry):
-        multiply(first, PANELS - 1, j, False)
+    diagonal = flip(chip, 3)
+
+    def near(j, carry):
+        receive(2, j)
+        for i in range(PANELS - 1):
+            @pl.when(first + i != diagonal)
+            def _():
+                multiply(first + i, 1, j, True)
+
         return carry
 
-    lax.fori_loop(0, pieces, early, 0)
+    lax.fori_loop(0, pieces, near, 0)
+    relay((3,))
+
+    @pl.when(diagonal != farthest)
+    def _():
+        def one(j, carry):
+            multiply(diagonal, 1, j, True)
+            return carry
+
+        lax.fori_loop(0, pieces, one, 0)
+
 
     def last(j, total):
         receive(rows_n - 1, j)
@@ -298,7 +317,7 @@
             pltpu.VMEM((PANELS, KP, col_block), jnp.float32),
             pltpu.VMEM((PANELS, row_block, KP), jnp.float32),
             pltpu.VMEM((PANELS, row_block, 2 * KP), jnp.bfloat16),
-            pltpu.VMEM((3 * KP * (PANELS - 1), col_block // pieces), jnp.bfloat16),
+            pltpu.VMEM((3 * KP, col_block // pieces), jnp.bfloat16),
             pltpu.VMEM((cols_n, 8, 128), jnp.float32),
             pltpu.VMEM((rows_n, 8, 128), jnp.float32),
             dma((2,)), dma((PANELS, pieces)), dma((PANELS, pieces)), dma((PANELS, pieces)),

time: 89.9 us -> 89.9 us (level)
  no operation moved by 1% of the time
where the time goes in v3:
time: 89.9 us; the launch traced here: 89.7 us
  Pallas kernels  84 us (93%)
  local copies, waits for them, and re-layouts  3.4 us (4%)
  between operations  2.33 us (3%)
    pallas_call x1, Pallas kernels, fused(): pl.pallas_call(functools.partial(kernel, rows_n, cols_n, order, pieces),...  84 us
    unnamed x1, local copies, waits for them, and re-layouts  3.4 us

profile of v3, /device:TPU:0, one launch (start us, length us, event | category | flops | bytes accessed | tf_op | source)
XLA Modules:
  0.0 89.7 jit_solution(3715522676877187753)
XLA Ops:
  0.6 84.0 %shard_map.30 = (f32[2048,1024]{1,0:T(8,128)S(1)}, f32[1,1]{1,0:T(1,128)}) custom-call(f32[2048,1024]{1,0:T(8,128)} %x_ref.1), custom_call_target="tpu_custom_call" | custom-call | tf_op jit(solution)/shard_map/pallas_call | solution.py:308
  84.6 3.4 %copy.5 = f32[2048,1024]{1,0:T(8,128)} copy(f32[2048,1024]{1,0:T(8,128)S(1)} %get-tuple-element.6) | data formatting | bytes 16777216
